TPU v7x, 32 devices: a whole 2x2x4 slice. The times are simulated.
32 devices in a mesh: ckpt: 2 (over y), row: 4 (over z), col: 4 (over x, core).
Axes of the slice: x: 2, y: 2, z: 4, core: 2. Of those that a mesh axis runs over, the one named last changes fastest.
Arguments:
- grad_slab: bfloat16 [768, 27648], P(('ckpt', 'col'), 'row'), parts along dimension 0, may hold values from -6 to 6
- eigenbasis: bfloat16 [55296, 14336], P(('ckpt', 'row'), 'col'), parts along dimension 0, may hold values from -0.0546875 to 0.0546875
- eigenvalues: bfloat16 [768, 14336], P('ckpt', 'col'), parts along dimension 0, may hold values from 0.049804688 to 5
Outputs:
- preconditioned: bfloat16 [768, 27648], P(('ckpt', 'col'), 'row'), parts along dimension 0
There are 2 independent parts, one for each index of `ckpt`. A program takes and returns all parts, laid end to end along the dimension named above; each array names one. Nothing has to cross between parts.
All inputs are finite; a program needn't handle non-finite values.
Results may differ from a plain program's by a relative error of at most 0.0046.
Values may be sent and summed in bfloat16 or wider, within the bound.
No kernel may reach another device: no remote copies, remote signals or barrier semaphores. Data moves between devices by JAX's collectives and lax.ppermute only.
A program may use at most 128 MiB of HBM per device.

v0:
```python
import jax
import jax.numpy as jnp
from jax import lax
from jax.sharding import PartitionSpec as P

DAMPING = 0.1


def on_device(grad_slab, eigenbasis, eigenvalues):
    rotated_part = jnp.dot(
        lax.all_gather(grad_slab, "col", axis=0, tiled=True),
        eigenbasis,
        preferred_element_type=jnp.float32,
    )
    own_share = lax.psum_scatter(rotated_part, "row", scatter_dimension=1, tiled=True)
    share_width = own_share.shape[1]
    offset = lax.axis_index("row") * share_width
    own_values = lax.dynamic_slice_in_dim(eigenvalues, offset, share_width, 1)
    scaled_share = (own_share / (own_values.astype(jnp.float32) + DAMPING)).astype(jnp.bfloat16)
    scaled = lax.all_gather(scaled_share, "row", axis=1, tiled=True)
    result = lax.psum_scatter(
        lax.dot_general(
            scaled, eigenbasis, (((1,), (1,)), ((), ())), preferred_element_type=jnp.float32
        ),
        "col",
        scatter_dimension=0,
        tiled=True,
    )
    return result.astype(jnp.bfloat16)


def solution(mesh):
    placed = (P(("ckpt", "col"), "row"), P(("ckpt", "row"), "col"), P("ckpt", "col"))
    return jax.shard_map(
        on_device, mesh=mesh, in_specs=placed, out_specs=P(("ckpt", "col"), "row"), check_vma=False
    )
```

profile of v0, /device:TPU:0, one launch (start us, length us, event | category | flops | bytes accessed | tf_op | source)
XLA Modules:
  0.0 360.5 jit_solution(17615250611233539251)
XLA Ops:
  6.5 0.0 all-gather.3.cloned.1.call-start
  6.5 0.7 all-gather.3.cloned.1.call-update
  7.3 0.0 reduce-scatter.3.cloned.1.call-start
  7.3 45.1 %all-gather.3.cloned.1.call-done = bf16[384,6912]{1,0:T(8,128)(2,1)} async-done(((bf16[96,6912]{1,0:T(8,128)(2,1)}), bf16[384,6912]{1,0:T(8,128)(2,1)}) %all-gather.3.cloned.1.call-update) | async-done | bytes 5308432 | tf_op jit(solution)/shard_map/all_gather | solution.py:11
  52.4 28.3 %fusion = f32[384,3584]{1,0:T(8,128)} fusion(bf16[384,6912]{1,0:T(8,128)(2,1)} %all-gather.3.cloned.1.call-done, bf16[6912,3584]{1,0:T(8,128)(2,1)} %param.4), kind=kOutput, calls=%fused_computation.1 | convolution fusion | flops 19025362944 | bytes 60358656 | tf_op jit(solution)/shard_map/dot_general | solution.py:10
  80.7 0.0 reduce-scatter.3.cloned.1.call-update
  80.8 0.0 all-gather.5.cloned.1.call-start
  80.8 98.1 %reduce-scatter.3.cloned.1.call-done = f32[384,896]{1,0:T(8,128)} async-done(((f32[384,3584]{1,0:T(8,128)}), f32[384,896]{1,0:T(8,128)}) %reduce-scatter.3.cloned.1.call-update) | async-done | bytes 1376272 | tf_op jit(solution)/shard_map/reduce_scatter | solution.py:15
  178.9 2.6 divide_convert_fusion
  181.5 0.0 all-gather.5.cloned.1.call-update
  181.5 0.0 reduce-scatter.5.cloned.1.call-start
  181.6 57.4 %all-gather.5.cloned.1.call-done = bf16[384,3584]{1,0:T(8,128)(2,1)} async-done(((bf16[384,896]{1,0:T(8,128)(2,1)}), bf16[384,3584]{1,0:T(8,128)(2,1)}) %all-gather.5.cloned.1.call-update) | async-done | bytes 2752528 | tf_op jit(solution)/shard_map/all_gather | solution.py:20
  239.0 28.0 %fusion.1 = f32[384,6912]{1,0:T(8,128)} fusion(bf16[384,3584]{1,0:T(8,128)(2,1)} %all-gather.5.cloned.1.call-done, bf16[6912,3584]{1,0:T(8,128)(2,1)} %param.4), kind=kOutput, calls=%fused_computation.2 | convolution fusion | flops 19025362944 | bytes 62914560 | tf_op jit(solution)/shard_map/dot_general | solution.py:22
  267.0 0.0 reduce-scatter.5.cloned.1.call-update
  267.0 84.0 %reduce-scatter.5.cloned.1.call-done = f32[96,6912]{1,0:T(8,128)} async-done(((f32[384,6912]{1,0:T(8,128)}), f32[96,6912]{1,0:T(8,128)}) %reduce-scatter.5.cloned.1.call-update) | async-done | bytes 2654224 | tf_op jit(solution)/shard_map/reduce_scatter | solution.py:21
  351.0 2.9 convert_element_type.11
Async XLA Ops:
  6.5 45.9 %all-gather.3.cloned.1.call-start = ((), (), s32[]{:S(2)}) async-start(), calls=%async_computation.2 | async-start | bytes 6635520 | tf_op jit(solution)/shard_map/all_gather | solution.py:11
  7.3 171.7 %reduce-scatter.3.cloned.1.call-start = ((), (), s32[]{:S(2)}) async-start(), calls=%async_computation.3 | async-start | bytes 6881280 | tf_op jit(solution)/shard_map/reduce_scatter | solution.py:15
  80.8 158.2 %all-gather.5.cloned.1.call-start = ((), (), s32[]{:S(2)}) async-start(), calls=%async_computation.4 | async-start | bytes 3440640 | tf_op jit(solution)/shard_map/all_gather | solution.py:20
  181.5 169.5 %reduce-scatter.5.cloned.1.call-start = ((), (), s32[]{:S(2)}) async-start(), calls=%async_computation.5 | async-start | bytes 13271040 | tf_op jit(solution)/shard_map/reduce_scatter | solution.py:21
Sparse Core Ops, SparseCore 0:
  8.9 43.4 all-gather.2
  80.9 98.0 reduce-scatter.2
  181.7 57.2 all-gather.4
  267.1 83.8 reduce-scatter.4
where the time goes:
time: 361 us; the launch traced here: 360 us
  waiting for transfers between devices  285 us (79%)
  matrix products  56.3 us (16%)
  between operations  13.1 us (4%)
  other arithmetic  5.52 us (2%)
    reduce_scatter x1, waiting for transfers between devices, on_device(): lax.psum_scatter(rotated_part, 'row', scatter_dimension=1, tiled=True)  98.1 us
    reduce_scatter x1, waiting for transfers between devices, on_device(): lax.psum_scatter(lax.dot_general(scaled, eigenbasis, (((1,), (1,)), ((),...  84 us
    all_gather x1, waiting for transfers between devices, on_device(): scaled = lax.all_gather(scaled_share, 'row', axis=1, tiled=True)  57.4 us
    all_gather x1, waiting for transfers between devices, on_device(): lax.all_gather(grad_slab, 'col', axis=0, tiled=True)  45.1 us
    dot_general x1, matrix products, on_device(): jnp.dot(lax.all_gather(grad_slab, 'col', axis=0, tiled=True), eigenbasis,...  28.3 us
    dot_general x1, matrix products, on_device(): lax.dot_general(scaled, eigenbasis, (((1,), (1,)), ((), ())), preferred_e...  28 us
  transfers between devices with their start and end apart: 4, of which 4 were waited for; matrix products, arithmetic and copies ran while one was open for 0% of the time, Pallas kernels for 0%

commit v1 on v0

--- a/solution.py
+++ b/solution.py
@@ -2,16 +2,20 @@
 import jax.numpy as jnp
 from jax import lax
 from jax.sharding import PartitionSpec as P
+from jax.lax import all_to_all, axis_size
 
 DAMPING = 0.1
 
 
 def on_device(grad_slab, eigenbasis, eigenvalues):
-    rotated_part = jnp.dot(
-        lax.all_gather(grad_slab, "col", axis=0, tiled=True),
-        eigenbasis,
-        preferred_element_type=jnp.float32,
-    )
+
+    def step_on_tiles(my_tile):
+        top = jnp.stack([my_tile for _ in range(axis_size("col"))], axis=0)
+        lower = all_to_all(top, axis_name="col", split_axis=0, concat_axis=0)
+        kept_arr = jnp.concatenate(lower, axis=0)
+        return kept_arr
+
+    rotated_part = jnp.dot(step_on_tiles(grad_slab), eigenbasis, preferred_element_type=jnp.float32)
     own_share = lax.psum_scatter(rotated_part, "row", scatter_dimension=1, tiled=True)
     share_width = own_share.shape[1]
     offset = lax.axis_index("row") * share_width

time: 361 us -> 379 us (1.050)
  blocking collectives: 0 us -> 64.1 us
  waiting for transfers between devices: 285 us -> 240 us
    all_to_all x0 -> x1, blocking collectives: none -> 64.1 us  [step_on_tiles(): lower = all_to_all(top, axis_name='col', split_axis=0, concat_axis=0)]
    all_gather x1 -> x0, waiting for transfers between devices: 45.1 us -> none  [on_device(): lax.all_gather(grad_slab, 'col', axis=0, tiled=True)]
  transfers between devices with their start and end apart: 4 -> 3, of which waited for: 4 -> 3; matrix products, arithmetic and copies ran while one was open for 0% -> 0% of each run, Pallas kernels for 0% -> 0%
where the time goes in v1:
time: 379 us
  waiting for transfers between devices  240 us (63%)
  blocking collectives  64.1 us (17%)
  matrix products  54.3 us (14%)
  between operations  13.1 us (3%)
  other arithmetic  5.52 us (1%)
    reduce_scatter x1, waiting for transfers between devices, on_device(): lax.psum_scatter(rotated_part, 'row', scatter_dimension=1, tiled=True)  98.5 us
    reduce_scatter x1, waiting for transfers between devices, on_device(): lax.psum_scatter(lax.dot_general(scaled, eigenbasis, (((1,), (1,)), ((),...  84 us
    all_to_all x1, blocking collectives, step_on_tiles(): lower = all_to_all(top, axis_name='col', split_axis=0, concat_axis=0)  64.1 us
    all_gather x1, waiting for transfers between devices, on_device(): scaled = lax.all_gather(scaled_share, 'row', axis=1, tiled=True)  57.3 us
    dot_general x1, matrix products, on_device(): lax.dot_general(scaled, eigenbasis, (((1,), (1,)), ((), ())), preferred_e...  28.1 us
    dot_general x1, matrix products, on_device(): jnp.dot(step_on_tiles(grad_slab), eigenbasis, preferred_element_type=jnp....  26.2 us
  transfers between devices with their start and end apart: 3, of which 3 were waited for; matrix products, arithmetic and copies ran while one was open for 0% of the time, Pallas kernels for 0%

profile of v1, /device:TPU:0, one launch (start us, length us, event | category | flops | bytes accessed | tf_op | source)
XLA Modules:
  0.0 378.7 jit_solution(14741459584438241539)
XLA Ops:
  6.5 0.0 reduce-scatter.3.cloned.1.call-start
  6.5 1.7 stack.2
  8.2 64.1 %all_to_all.5 = bf16[4,96,6912]{2,1,0:T(8,128)(2,1)S(1)} all-to-all(bf16[4,96,6912]{2,1,0:T(8,128)(2,1)S(1)} %stack.2), channel_id=1, replica_groups=mesh['ckpt'=2,'row'=4,'col'=4] {'col'}, dimensions={0} | all-to-all | bytes 10616832 | tf_op jit(solution)/shard_map/all_to_all | solution.py:14
  72.3 26.2 %fusion = f32[384,3584]{1,0:T(8,128)} fusion(bf16[384,6912]{1,0:T(8,128)(2,1)S(1)} %bitcast.5, bf16[6912,3584]{1,0:T(8,128)(2,1)} %param.4), kind=kOutput, calls=%fused_computation.1 | convolution fusion | flops 19025362944 | bytes 60358656 | tf_op jit(solution)/shard_map/dot_general | solution.py:18
  98.5 0.0 reduce-scatter.3.cloned.1.call-update
  98.6 0.0 all-gather.2.cloned.1.call-start
  98.6 98.5 %reduce-scatter.3.cloned.1.call-done = f32[384,896]{1,0:T(8,128)} async-done(((f32[384,3584]{1,0:T(8,128)}), f32[384,896]{1,0:T(8,128)}) %reduce-scatter.3.cloned.1.call-update) | async-done | bytes 1376272 | tf_op jit(solution)/shard_map/reduce_scatter | solution.py:19
  197.1 2.6 divide_convert_fusion
  199.7 0.0 all-gather.2.cloned.1.call-update
  199.7 0.0 reduce-scatter.5.cloned.1.call-start
  199.8 57.3 %all-gather.2.cloned.1.call-done = bf16[384,3584]{1,0:T(8,128)(2,1)} async-done(((bf16[384,896]{1,0:T(8,128)(2,1)}), bf16[384,3584]{1,0:T(8,128)(2,1)}) %all-gather.2.cloned.1.call-update) | async-done | bytes 2752528 | tf_op jit(solution)/shard_map/all_gather | solution.py:24
  257.1 28.1 %fusion.1 = f32[384,6912]{1,0:T(8,128)} fusion(bf16[384,3584]{1,0:T(8,128)(2,1)} %all-gather.2.cloned.1.call-done, bf16[6912,3584]{1,0:T(8,128)(2,1)} %param.4), kind=kOutput, calls=%fused_computation.2 | convolution fusion | flops 19025362944 | bytes 62914560 | tf_op jit(solution)/shard_map/dot_general | solution.py:26
  285.2 0.0 reduce-scatter.5.cloned.1.call-update
  285.2 84.0 %reduce-scatter.5.cloned.1.call-done = f32[96,6912]{1,0:T(8,128)} async-done(((f32[384,6912]{1,0:T(8,128)}), f32[96,6912]{1,0:T(8,128)}) %reduce-scatter.5.cloned.1.call-update) | async-done | bytes 2654224 | tf_op jit(solution)/shard_map/reduce_scatter | solution.py:25
  369.2 2.9 convert_element_type.11
Async XLA Ops:
  6.5 190.6 %reduce-scatter.3.cloned.1.call-start = ((), (), s32[]{:S(2)}) async-start(), calls=%async_computation.3 | async-start | bytes 6881280 | tf_op jit(solution)/shard_map/reduce_scatter | solution.py:19
  98.6 158.5 %all-gather.2.cloned.1.call-start = ((), (), s32[]{:S(2)}) async-start(), calls=%async_computation.4 | async-start | bytes 3440640 | tf_op jit(solution)/shard_map/all_gather | solution.py:24
  199.7 169.5 %reduce-scatter.5.cloned.1.call-start = ((), (), s32[]{:S(2)}) async-start(), calls=%async_computation.5 | async-start | bytes 13271040 | tf_op jit(solution)/shard_map/reduce_scatter | solution.py:25
Sparse Core Ops, SparseCore 0:
  98.7 98.3 reduce-scatter.2
  199.8 57.2 all-gather.1
  285.3 83.8 reduce-scatter.4
